TPU v7x, 32 devices: a whole 2x2x4 slice. The times are simulated.
32 devices in a mesh: vocab: 8 (over y, x, core), dp: 4 (over z).
Axes of the slice: x: 2, y: 2, z: 4, core: 2. Of those that a mesh axis runs over, the one named last changes fastest.
Arguments:
- token_ids: int32 [8192], P(('vocab', 'dp')), may hold values from 0 to 50256
- target_ids: int32 [8192], P(('vocab', 'dp')), may hold values from 0 to 50256
- loss_mask: int32 [8192], P(('vocab', 'dp')), may hold values from 0 to 1, as said below
- seq_ids: int32 [8192], P(('vocab', 'dp')), may hold values from 0 to 255, as said below
- embed_table: bfloat16 [50304, 1024], P('vocab'), may hold values from -0.359375 to 0.359375
- pos_table: bfloat16 [1024, 1024], replicated, may hold values from -0.359375 to 0.359375
- gains: float32 [3, 1024], replicated, may hold values from 0.5 to 1.5
- shifts: float32 [3, 1024], replicated, may hold values from -1.8 to 1.8
- linear_bias: float32 [1, 9216], replicated, may hold values from -1.8 to 1.8
- query_key_value_weight: bfloat16 [1, 1024, 3072], replicated, may hold values from -0.1875 to 0.1875
- w_out: bfloat16 [1, 1024, 1024], replicated, may hold values from -0.5 to 0.5
- w_fc: bfloat16 [1, 1024, 4096], replicated, may hold values from -0.1875 to 0.1875
- w_proj: bfloat16 [1, 4096, 1024], replicated, may hold values from -0.09375 to 0.09375
- adapters: float32 [1, 24576], P(None, 'vocab'), may hold values from -0.18 to 0.18
- first_moment: float32 [1, 24576], P(None, 'vocab'), may hold values from -4.2483338e-05 to 4.2483338e-05
- second_moment: float32 [1, 24576], P(None, 'vocab'), may hold values from 2.0345052e-12 to 3.2552083e-11
- step_count: int32 [1], replicated, may hold values from 2 to 20
Outputs:
- loss: float32 [], replicated
- grad_norm: float32 [], replicated
- new_adapters: float32 [1, 24576], P(None, 'vocab')
- new_first: float32 [1, 24576], P(None, 'vocab')
- new_second: float32 [1, 24576], P(None, 'vocab')
- adapter_copy: bfloat16 [1, 24576], P(None, 'vocab')
Inputs may be any that keep to these rules, and one draw needn't show every extreme that they name: seq_ids never falls; the tokens of each device form whole sequences of 256 // 8 times 1, 2, 4 or 8 tokens, each starting at a multiple of its length within the device; some device holds one sequence of 256 tokens and some device eight of 32. `token_ids`: every id is a real row, below 50257. `target_ids`: every target is a real row, below 50257. `loss_mask`: the share of ones differs from device to device; some devices have all ones.
All inputs are finite; a program needn't handle non-finite values.
Results may differ from a plain program's by a relative error of at most 0.0051.
Values may be sent and summed in bfloat16 or wider, within the bound.
A program may use at most 256 MiB of HBM per device.

v0:
```python
import jax
import jax.numpy as jnp
from jax import lax
from jax.sharding import PartitionSpec as P

MODEL_WIDTH = 1024
HEADS = 16
HEAD_DIM = 64
FF = 4096
VOCAB_REAL = 50257
RANK = 4
LAYERS = 1
TOK_DEV = 256


PRECISE = lax.Precision.HIGHEST
ADAPTER_SCALE = 8.0
CLIP_NORM = 0.01
BETA_ONE = 0.9
BETA_TWO = 0.999
ADAM_EPS = 1e-08
WEIGHT_DECAY = 0.01
LEARN_RATE = 0.02


def mixed_product(left, right):
    return jnp.dot(left, right, preferred_element_type=jnp.float32)


def exact_product(left, right):
    return jnp.dot(left.astype(jnp.float32), right.astype(jnp.float32), precision=PRECISE)


def layer_norm(values, gain, shift):
    center = values - jnp.mean(values, -1, keepdims=True)
    spread = jnp.mean(center * center, -1, keepdims=True)
    inverse = lax.rsqrt(spread + 1e-05)
    normed = center * inverse
    return (normed * gain + shift, normed, inverse)


def norm_back(grad_in, normed, inverse, gain):
    scaled = grad_in * gain
    return inverse * (
        scaled
        - jnp.mean(scaled, -1, keepdims=True)
        - normed * jnp.mean(scaled * normed, -1, keepdims=True)
    )


def gelu(values):
    return (
        0.5
        * values
        * (1.0 + jnp.tanh(0.7978845608028654 * (values + 0.044715 * values * values * values)))
    )


def positions_of(seq):
    place = jnp.arange(seq.shape[0], dtype=jnp.int32)
    fresh = jnp.concatenate([jnp.ones((1,), bool), seq[1:] != seq[:-1]])
    start = lax.cummax(jnp.where(fresh, place, 0))
    return place - start


def split_adapter(flat):
    width = MODEL_WIDTH * RANK
    qkv_down_matrix = flat[:width].reshape(MODEL_WIDTH, RANK)
    output_down_matrix = flat[width : 2 * width].reshape(MODEL_WIDTH, RANK)
    qkv_up_matrix = flat[2 * width : 5 * width].reshape(RANK, 3 * MODEL_WIDTH)
    output_up_matrix = flat[5 * width :].reshape(RANK, MODEL_WIDTH)
    return (qkv_down_matrix, output_down_matrix, qkv_up_matrix, output_up_matrix)


def split_heads(query_key_value):
    count = query_key_value.shape[0]
    query = query_key_value[:, :MODEL_WIDTH].reshape(count, HEADS, HEAD_DIM)
    keys = query_key_value[:, MODEL_WIDTH : 2 * MODEL_WIDTH].reshape(count, HEADS, HEAD_DIM)
    values = query_key_value[:, 2 * MODEL_WIDTH :].reshape(count, HEADS, HEAD_DIM)
    return (query, keys, values)


def attention_forward(query_key_value, visible):
    query, keys, values = split_heads(query_key_value)
    scores = jnp.einsum("qhd,khd->hqk", query, keys, preferred_element_type=jnp.float32) * 0.125
    scores = jnp.where(visible[None], scores, -1e30)
    row_top = jnp.max(scores, -1, keepdims=True)
    expd = jnp.exp(scores - row_top)
    row_total = jnp.sum(expd, -1, keepdims=True)
    probs = (expd / row_total).astype(jnp.bfloat16)
    attention_output = jnp.einsum("hqk,khd->qhd", probs, values, preferred_element_type=jnp.float32)
    return (
        attention_output.reshape(query_key_value.shape[0], MODEL_WIDTH),
        row_top + jnp.log(row_total),
    )


def attention_back(query_key_value, visible, row_lse, attention_output_gradient):
    query, keys, values = split_heads(query_key_value)
    count = query_key_value.shape[0]
    scores = jnp.einsum("qhd,khd->hqk", query, keys, preferred_element_type=jnp.float32) * 0.125
    probs = jnp.where(visible[None], jnp.exp(scores - row_lse), 0.0)
    grad_heads = attention_output_gradient.reshape(count, HEADS, HEAD_DIM)
    grad_probs = jnp.einsum("qhd,khd->hqk", grad_heads, values, preferred_element_type=jnp.float32)
    grad_values = jnp.einsum(
        "hqk,qhd->khd", probs.astype(jnp.bfloat16), grad_heads, preferred_element_type=jnp.float32
    )
    grad_scores = probs * (grad_probs - jnp.sum(probs * grad_probs, -1, keepdims=True))
    grad_scores = grad_scores.astype(jnp.bfloat16)
    grad_query = (
        jnp.einsum("hqk,khd->qhd", grad_scores, keys, preferred_element_type=jnp.float32) * 0.125
    )
    grad_keys = (
        jnp.einsum("hqk,qhd->khd", grad_scores, query, preferred_element_type=jnp.float32) * 0.125
    )
    joined = jnp.concatenate(
        [
            grad_query.reshape(count, MODEL_WIDTH),
            grad_keys.reshape(count, MODEL_WIDTH),
            grad_values.reshape(count, MODEL_WIDTH),
        ],
        axis=1,
    )
    return joined.astype(jnp.bfloat16)


def local(
    token_ids,
    target_ids,
    loss_mask,
    seq_ids,
    embed_table,
    pos_table,
    gains,
    shifts,
    linear_bias,
    query_key_value_weight,
    w_out,
    w_fc,
    w_proj,
    adapters,
    first_moment,
    second_moment,
    step_count,
):
    vocab_place = lax.axis_index("vocab")
    vocab_count = lax.axis_size("vocab")
    total_tokens = TOK_DEV * vocab_count * lax.axis_size("dp")
    shard_rows = embed_table.shape[0]
    all_tokens, all_targets, all_mask = (
        lax.all_gather(token_ids, "vocab", axis=0, tiled=True),
        lax.all_gather(target_ids, "vocab", axis=0, tiled=True),
        lax.all_gather(loss_mask, "vocab", axis=0, tiled=True),
    )
    mask_weights = all_mask.astype(jnp.float32)
    wanted = all_tokens - vocab_place * shard_rows
    inside = (wanted >= 0) & (wanted < shard_rows)
    picked_rows = jnp.take(embed_table, jnp.clip(wanted, 0, shard_rows - 1), axis=0)
    embedded = lax.psum_scatter(
        jnp.where(inside[:, None], picked_rows.astype(jnp.float32), 0.0).astype(jnp.bfloat16),
        "vocab",
        scatter_dimension=0,
        tiled=True,
    ).astype(jnp.float32)
    copies = lax.all_gather(adapters.astype(jnp.bfloat16), "vocab", axis=1, tiled=True)
    resid = embedded + pos_table[positions_of(seq_ids)].astype(jnp.float32)
    place = jnp.arange(TOK_DEV)
    visible = (seq_ids[:, None] == seq_ids[None, :]) & (place[None, :] <= place[:, None])
    layer_params = 0
    qkv_down_matrix, output_down_matrix, qkv_up_matrix, output_up_matrix = split_adapter(
        copies[layer_params]
    )
    bias_vector = linear_bias[layer_params]
    hidden_first, normed_one, inverse_one = layer_norm(
        resid, gains[2 * layer_params], shifts[2 * layer_params]
    )
    hidden_first = hidden_first.astype(jnp.bfloat16)
    adapter_input = mixed_product(hidden_first, qkv_down_matrix).astype(jnp.bfloat16)
    query_key_value = (
        mixed_product(hidden_first, query_key_value_weight[layer_params])
        + bias_vector[: 3 * MODEL_WIDTH]
        + ADAPTER_SCALE * mixed_product(adapter_input, qkv_up_matrix)
    )
    query_key_value = query_key_value.astype(jnp.bfloat16)
    attention_output, row_lse = attention_forward(query_key_value, visible)
    attention_output = attention_output.astype(jnp.bfloat16)
    adapter_middle = mixed_product(attention_output, output_down_matrix).astype(jnp.bfloat16)
    resid = (
        resid
        + mixed_product(attention_output, w_out[layer_params])
        + bias_vector[3 * MODEL_WIDTH : 4 * MODEL_WIDTH]
        + ADAPTER_SCALE * mixed_product(adapter_middle, output_up_matrix)
    )
    h_two, normed_two, inverse_two = layer_norm(
        resid, gains[2 * layer_params + 1], shifts[2 * layer_params + 1]
    )
    h_two = h_two.astype(jnp.bfloat16)
    pre = (
        mixed_product(h_two, w_fc[layer_params])
        + bias_vector[4 * MODEL_WIDTH : 4 * MODEL_WIDTH + FF]
    )
    act = gelu(pre).astype(jnp.bfloat16)
    resid = resid + mixed_product(act, w_proj[layer_params]) + bias_vector[4 * MODEL_WIDTH + FF :]
    saved = [
        (
            hidden_first,
            normed_one,
            inverse_one,
            adapter_input,
            query_key_value,
            row_lse,
            attention_output,
            adapter_middle,
            normed_two,
            inverse_two,
            pre,
        )
    ]
    hidden, normed_last, inverse_last = layer_norm(resid, gains[2 * LAYERS], shifts[2 * LAYERS])
    hidden = hidden.astype(jnp.bfloat16)
    columns = vocab_place * shard_rows + jnp.arange(shard_rows)
    live = columns < VOCAB_REAL

    def head_logits(row_block):
        logits = jnp.einsum("td,vd->tv", row_block, embed_table, preferred_element_type=jnp.float32)
        return jnp.where(live[None], logits, -1e30)

    piece = lax.all_gather(hidden, "vocab", axis=0, tiled=True)
    logits = head_logits(piece)
    row_top = jnp.max(logits, -1)
    row_total = jnp.sum(jnp.exp(logits - row_top[:, None]), -1)
    wanted = all_targets
    picked = jnp.sum(jnp.where(columns[None, :] == wanted[:, None], logits, 0.0), -1)
    gathered, row_top, row_total, picked = (piece, row_top, row_total, picked)
    joint_top = lax.pmax(row_top, "vocab")
    row_total = row_total * jnp.exp(row_top - joint_top)
    row_total, picked = lax.psum((row_total, picked), "vocab")
    row_lse = joint_top + jnp.log(row_total)
    loss_part = jnp.sum(mask_weights * (row_lse - picked))
    row_block = gathered
    logits = head_logits(row_block)
    wanted = all_targets
    hit = (columns[None, :] == wanted[:, None]).astype(jnp.float32)
    grad_logits = (
        mask_weights[:, None] * (jnp.exp(logits - row_lse[:, None]) - hit) * (1.0 / total_tokens)
    ).astype(jnp.bfloat16)
    grad_hidden = lax.psum_scatter(
        mixed_product(grad_logits, embed_table), "vocab", scatter_dimension=0, tiled=True
    )
    grad_resid = norm_back(grad_hidden, normed_last, inverse_last, gains[2 * LAYERS])
    layer_grads = []
    for layer_params in reversed(range(LAYERS)):
        (
            hidden_first,
            normed_one,
            inverse_one,
            adapter_input,
            query_key_value,
            row_lse_l,
            attention_output,
            adapter_middle,
            normed_two,
            inverse_two,
            pre,
        ) = saved[layer_params]
        qkv_down_matrix, output_down_matrix, qkv_up_matrix, output_up_matrix = split_adapter(
            copies[layer_params]
        )
        grad_top = grad_resid.astype(jnp.bfloat16)
        grad_act = jnp.einsum(
            "te,fe->tf", grad_top, w_proj[layer_params], preferred_element_type=jnp.float32
        )
        grad_pre = jax.vjp(gelu, pre)[1](grad_act)[0].astype(jnp.bfloat16)
        grad_h_two = jnp.einsum(
            "tf,df->td", grad_pre, w_fc[layer_params], preferred_element_type=jnp.float32
        )
        grad_resid = grad_resid + norm_back(
            grad_h_two, normed_two, inverse_two, gains[2 * layer_params + 1]
        )
        middle_gradient = grad_resid.astype(jnp.bfloat16)
        adapter_middle_gradient = ADAPTER_SCALE * jnp.einsum(
            "te,re->tr", middle_gradient, output_up_matrix, preferred_element_type=jnp.float32
        )
        output_up_gradient = ADAPTER_SCALE * jnp.einsum(
            "iz,iq->zq", adapter_middle, middle_gradient, preferred_element_type=jnp.float32
        )
        output_down_gradient = exact_product(attention_output.T, adapter_middle_gradient)
        attention_output_gradient = jnp.einsum(
            "te,de->td", middle_gradient, w_out[layer_params], preferred_element_type=jnp.float32
        )
        attention_output_gradient = (
            attention_output_gradient + exact_product(adapter_middle_gradient, output_down_matrix.T)
        ).astype(jnp.bfloat16)
        query_key_value_gradient = attention_back(
            query_key_value, visible, row_lse_l, attention_output_gradient
        )
        qkv_up_gradient = ADAPTER_SCALE * jnp.einsum(
            "iz,iq->zq", adapter_input, query_key_value_gradient, preferred_element_type=jnp.float32
        )
        adapter_input_gradient = ADAPTER_SCALE * jnp.einsum(
            "te,re->tr", query_key_value_gradient, qkv_up_matrix, preferred_element_type=jnp.float32
        )
        qkv_down_gradient = exact_product(hidden_first.T, adapter_input_gradient)
        layer_grads.insert(
            0,
            jnp.concatenate(
                [
                    qkv_down_gradient.reshape(-1),
                    output_down_gradient.reshape(-1),
                    qkv_up_gradient.reshape(-1),
                    output_up_gradient.reshape(-1),
                ]
            ),
        )
    local_grads = jnp.stack(layer_grads)
    grad_shard = lax.psum_scatter(local_grads, "vocab", scatter_dimension=1, tiled=True)
    grad_shard, loss_sum = lax.psum((grad_shard, loss_part), "dp")
    square_sum = lax.psum(jnp.sum(grad_shard * grad_shard), "vocab")
    loss = loss_sum / total_tokens
    grad_norm = jnp.sqrt(square_sum)
    clipped = grad_shard * jnp.minimum(1.0, CLIP_NORM / (grad_norm + 1e-06))
    step = step_count[0].astype(jnp.float32)
    new_first = BETA_ONE * first_moment + (1.0 - BETA_ONE) * clipped
    new_second = BETA_TWO * second_moment + (1.0 - BETA_TWO) * clipped * clipped
    fix_one = 1.0 - jnp.power(BETA_ONE, step)
    fix_two = 1.0 - jnp.power(BETA_TWO, step)
    motion = (
        new_first / fix_one / (jnp.sqrt(new_second / fix_two) + ADAM_EPS) + WEIGHT_DECAY * adapters
    )
    new_adapters = adapters - LEARN_RATE * motion
    return (loss, grad_norm, new_adapters, new_first, new_second, new_adapters.astype(jnp.bfloat16))


def solution(mesh):
    in_specs = (
        P(("vocab", "dp")),
        P(("vocab", "dp")),
        P(("vocab", "dp")),
        P(("vocab", "dp")),
        P("vocab", None),
        P(),
        P(),
        P(),
        P(),
        P(),
        P(),
        P(),
        P(),
        P(None, "vocab"),
        P(None, "vocab"),
        P(None, "vocab"),
        P(),
    )
    out_specs = (P(), P(), P(None, "vocab"), P(None, "vocab"), P(None, "vocab"), P(None, "vocab"))
    return jax.shard_map(local, mesh=mesh, in_specs=in_specs, out_specs=out_specs, check_vma=False)
```

profile of v0, /device:TPU:0, one launch (start us, length us, event | category | flops | bytes accessed | tf_op | source)
XLA Modules:
  0.0 552.7 jit_solution(14179724216567743253)
XLA Ops:
  7.2 10.7 %all-gather.1 = s32[8,1,256]{2,1,0:T(1,128)S(1)} all-gather(s32[1,1,256]{2,1,0:T(1,128)} %bitcast.172), channel_id=1, replica_groups=mesh['vocab'=8,'dp'=4] {'vocab'}, dimensions={0}, use_global_device_ids=true | all-gather | bytes 9216 | tf_op jit(solution)/shard_map/all_gather | solution.py:151
  18.0 17.3 %gather_fusion = bf16[2048,1024]{1,0:T(8,128)(2,1)} fusion(bf16[6288,1024]{1,0:T(8,128)(2,1)} %param.21, s32[2048]{0:T(1024)S(1)} %fusion.86), kind=kCustom, calls=%fused_computation | custom fusion | bytes 8396800 | tf_op jit(solution)/shard_map/jit(_take)/gather | solution.py:158
  35.3 4.1 select_convert_fusion
  40.7 9.3 %all_gather.17 = bf16[1,24576]{1,0:T(2,128)(2,1)S(1)} all-gather(bf16[1,3072]{1,0:T(2,128)(2,1)S(1)} %convert_element_type.95), channel_id=1, replica_groups=mesh['vocab'=8,'dp'=4] {'vocab'}, dimensions={1}, use_global_device_ids=true | all-gather | bytes 55296 | tf_op jit(solution)/shard_map/all_gather | solution.py:165
  51.7 3.6 gather_fusion.1
  55.4 35.5 %reduce-scatter.6.cloned.1.call-done = bf16[256,1024]{1,0:T(8,128)(2,1)} async-done(((bf16[2048,1024]{1,0:T(8,128)(2,1)}), bf16[256,1024]{1,0:T(8,128)(2,1)}) %reduce-scatter.6.cloned.1.call-update) | async-done | bytes 524304 | tf_op jit(solution)/shard_map/reduce_scatter | solution.py:159
  90.9 1.3 fusion.77
  92.2 1.3 multiply_reduce_fusion.5
  93.6 1.3 add_convert_fusion.3
  95.1 4.6 fusion.27
  100.4 1.2 fusion.107
  101.6 1.2 copy.47
  102.9 2.2 copy.46
  105.1 2.0 copy.45
  107.1 1.9 select_reduce_fusion.1
  109.1 0.9 fusion.33
  110.0 1.2 fusion.71
  111.6 0.7 fusion.54
  113.1 1.6 slice-done.5
  114.7 2.7 fusion.17
  117.5 2.8 fusion.112
  120.6 1.1 add_convert_fusion.1
  121.7 8.9 %all-gather = s32[8,1,256]{2,1,0:T(1,128)S(1)} all-gather(s32[1,1,256]{2,1,0:T(1,128)S(1)} %bitcast.173), channel_id=1, replica_groups=mesh['vocab'=8,'dp'=4] {'vocab'}, dimensions={0}, use_global_device_ids=true | all-gather | bytes 9216 | tf_op jit(solution)/shard_map/all_gather | solution.py:153
  130.6 8.1 %all-gather.2 = s32[8,1,256]{2,1,0:T(1,128)S(1)} all-gather(s32[1,1,256]{2,1,0:T(1,128)S(1)} %bitcast.174), channel_id=1, replica_groups=mesh['vocab'=8,'dp'=4] {'vocab'}, dimensions={0}, use_global_device_ids=true | all-gather | bytes 9216 | tf_op jit(solution)/shard_map/all_gather | solution.py:152
  138.8 19.6 %all-gather.5.cloned.1.call-done = bf16[2048,1024]{1,0:T(8,128)(2,1)} async-done(((bf16[256,1024]{1,0:T(8,128)(2,1)}), bf16[2048,1024]{1,0:T(8,128)(2,1)}) %all-gather.5.cloned.1.call-update) | async-done | bytes 4194320 | tf_op jit(solution)/shard_map/all_gather | solution.py:228
  158.4 35.7 %select_reduce_fusion = (f32[2048]{0:T(1024)S(1)}, f32[2048,6288]{0,1:T(8,128)}) fusion(pred[6288]{0:T(1024)(128)(4,1)S(1)} %broadcast_compare_fusion, bf16[2048,1024]{1,0:T(8,128)(2,1)} %all-gather.5.cloned.1.call-done, bf16[6288,1024]{1,0:T(8,128)(2,1)} %param.21), kind=kOutput, calls=%fused_computation.10 | convolution fusion | flops 26399537152 | bytes 68597904 | tf_op jit(solution)/shard_map/td,vd->tv/dot_general | solution.py:225
  194.1 13.3 %pmax.7 = f32[2048]{0:T(1024)S(1)} all-reduce(f32[2048]{0:T(1024)S(1)} %get-tuple-element.38), channel_id=1, replica_groups=mesh['vocab'=8,'dp'=4] {'vocab'}, use_global_device_ids=true, to_apply=%region_12.13 | all-reduce | flops 2048 | bytes 16384 | tf_op jit(solution)/shard_map/pmax | solution.py:235
  207.5 20.5 %fusion = (f32[2048]{0:T(1024)S(1)}, f32[2048]{0:T(1024)S(1)}) fusion(f32[2048,6288]{0,1:T(8,128)} %get-tuple-element.39, s32[2048]{0:T(1024)S(1)} %bitcast.159, s32[6288]{0:T(1024)S(1)} %iota_add_fusion, pred[6288]{0:T(1024)(128)(4,1)S(1)} %broadcast_compare_fusion, f32[2048]{0:T(1024)S(1)} %get-tuple-element.38), kind=kLoop, calls=%fused_computation.4 | loop fusion | flops 77262848 | bytes 51575504 | tf_op jit(solution)/shard_map/reduce_sum | solution.py:233
  227.9 12.5 %psum.35 = f32[2048]{0:T(1024)S(1)} all-reduce(f32[2048]{0:T(1024)S(1)} %exponential_multiply_fusion), channel_id=1, replica_groups=mesh['vocab'=8,'dp'=4] {'vocab'}, use_global_device_ids=true, to_apply=%region_14.15 | all-reduce | flops 2048 | bytes 16384 | tf_op jit(solution)/shard_map/psum | solution.py:237
  240.4 52.9 %fusion.5 = f32[2048,1024]{1,0:T(8,128)} fusion(bf16[6288,1024]{1,0:T(8,128)(2,1)} %param.21, f32[2048,6288]{0,1:T(8,128)} %get-tuple-element.39, f32[2048]{0:T(1024)S(1)} %log_add_fusion.1, f32[2048]{0:T(1024)S(1)} %bitcast.161, s32[2048]{0:T(1024)S(1)} %bitcast.160, s32[6288]{0:T(1024)S(1)} %iota_add_fusion, pred[6288]{0:T(1024)(128)(4,1)S(1)} %broadcast_compare_fusion), kind=kOutput, calls=%fused_computation.11 | convolution fusion | flops 26476806144 | bytes 72833744 | tf_op jit(solution)/shard_map/dot_general | solution.py:27
  293.5 71.7 %reduce-scatter.8.cloned.1.call-done = f32[256,1024]{1,0:T(8,128)} async-done(((f32[2048,1024]{1,0:T(8,128)}), f32[256,1024]{1,0:T(8,128)}) %reduce-scatter.8.cloned.1.call-update) | async-done | bytes 1048592 | tf_op jit(solution)/shard_map/reduce_scatter | solution.py:247
  365.1 1.5 multiply_reduce_fusion.6
  366.7 14.3 %fusion.104 = (f32[256]{0:T(256)S(1)}, f32[256]{0:T(256)S(1)}, f32[256,1024]{1,0:T(8,128)}) fusion(f32[256]{0:T(256)S(1)} %add_rsqrt_fusion.1, f32[256,1024]{1,0:T(8,128)} %copy-done.3, f32[256]{0:T(256)S(1)} %broadcast_multiply_fusion.5, f32[1024]{0:T(1024)S(1)} %bitcast.169, bf16[1,1024,4096]{2,1,0:T(8,128)(2,1)} %param.28, f32[256,4096]{1,0:T(8,128)} %copy-done.33, ...), kind=kOutput, calls=%fused_computation.162 | convolution fusion | flops 4323803136 | bytes 25182208 | tf_op jit(solution)/shard_map/tf,df->td/dot_general | solution.py:274
  381.0 2.5 add_convert_fusion
  384.0 0.7 fusion.37
  384.8 1.4 fusion.118
  386.1 1.5 fusion.68
  387.6 1.2 copy.49
  388.9 3.2 fusion.72
  392.3 1.4 multiply_reduce_fusion
  393.7 1.2 multiply_convert_fusion
  394.9 0.8 fusion.70
  398.5 6.8 %copy.61 = f32[1,24576]{0,1:T(8,128)} copy(f32[1,24576]{1,0:T(1,128)S(1)} %bitcast.147) | data formatting | bytes 196608
  406.1 91.7 %reduce-scatter.10.cloned.1.call-done = f32[3072,1]{1,0:T(8,128)} async-done(((f32[24576,1]{1,0:T(8,128)}), f32[3072,1]{1,0:T(8,128)}) %reduce-scatter.10.cloned.1.call-update) | async-done | bytes 12304
  497.8 1.9 copy.62
  499.6 18.7 %psum.38 = f32[1,3072]{1,0:T(1,128)S(1)} all-reduce(f32[1,3072]{1,0:T(1,128)S(1)} %copy.62), channel_id=1, replica_groups=mesh['vocab'=8,'dp'=4] {'dp'}, use_global_device_ids=true, to_apply=%region_26.27 | all-reduce | flops 3072 | bytes 24576 | tf_op jit(solution)/shard_map/psum | solution.py:317
  518.9 13.0 %all-reduce = (f32[2048]{0:T(1024)S(1)}, f32[]{:T(128)}) all-reduce(f32[2048]{0:T(1024)S(1)} %get-tuple-element.6, f32[]{:T(128)} %multiply_reduce_fusion.7), channel_id=1, replica_groups=mesh['vocab'=8,'dp'=4] {'vocab'}, use_global_device_ids=true, to_apply=%region_16.17 | all-reduce | flops 2049 | bytes 16392 | tf_op jit(solution)/shard_map/psum | solution.py:237
  533.2 9.0 %psum.37 = f32[]{:T(128)} all-reduce(f32[]{:T(128)} %multiply_reduce_fusion.8), channel_id=1, replica_groups=mesh['vocab'=8,'dp'=4] {'dp'}, use_global_device_ids=true, to_apply=%region_18.19 | all-reduce | flops 1 | bytes 8 | tf_op jit(solution)/shard_map/psum | solution.py:317
  (149 shorter events, 10.9 us)
Async XLA Ops:
  7.2 104.3 %copy-start = (bf16[1,1024,1024]{2,1,0:T(8,128)(2,1)S(1)}, bf16[1,1024,1024]{2,1,0:T(8,128)(2,1)}, u32[]{:S(2)}) copy-start(bf16[1,1024,1024]{2,1,0:T(8,128)(2,1)} %param.27) | copy-start | bytes 6291460
  7.2 83.8 %reduce-scatter.6.cloned.1.call-start = ((), (), s32[]{:S(2)}) async-start(), calls=%async_computation.3 | async-start | bytes 4718592 | tf_op jit(solution)/shard_map/reduce_scatter | solution.py:159
  39.4 0.7 copy-start.24
  39.4 1.3 copy-start.21
  39.4 15.8 %copy-start.23 = (f32[1,9216]{1,0:T(1,128)S(1)}, f32[1,9216]{1,0:T(1,128)}, u32[]{:S(2)}) copy-start(f32[1,9216]{1,0:T(1,128)} %param.25) | copy-start | bytes 110596
  39.4 15.8 %copy-start.27 = (f32[3,1024]{1,0:T(4,128)S(1)}, f32[3,1024]{1,0:T(4,128)}, u32[]{:S(2)}) copy-start(f32[3,1024]{1,0:T(4,128)} %param.23) | copy-start | bytes 36868
  39.4 15.8 %copy-start.28 = (f32[3,1024]{1,0:T(4,128)S(1)}, f32[3,1024]{1,0:T(4,128)}, u32[]{:S(2)}) copy-start(f32[3,1024]{1,0:T(4,128)} %param.24) | copy-start | bytes 36868
  39.5 118.9 %all-gather.5.cloned.1.call-start = ((), (), s32[]{:S(2)}) async-start(), calls=%async_computation.4 | async-start | bytes 4718592 | tf_op jit(solution)/shard_map/all_gather | solution.py:228
  50.1 49.7 %copy-start.19 = (bf16[4,3072]{1,0:T(4,128)(2,1)}, bf16[4,3072]{1,0:T(4,128)(2,1)S(1)}, u32[]{:S(2)}) copy-start(bf16[4,3072]{1,0:T(4,128)(2,1)S(1)} %reshape.265) | copy-start | bytes 73732
  50.8 60.4 %copy-start.12 = (bf16[1024,4]{1,0:T(8,128)(2,1)}, bf16[1024,4]{1,0:T(8,128)(2,1)S(1)}, u32[]{:S(2)}) copy-start(bf16[1024,4]{1,0:T(8,128)(2,1)S(1)} %reshape.269) | copy-start | bytes 24580
  51.6 43.5 %slice-start = ((f32[1,9216]{1,0:T(1,128)}), f32[1,3072]{1,0:T(1,128)S(1)}, s32[]{:S(2)}) async-start(f32[1,9216]{1,0:T(1,128)} %param.25), calls=%async_computation.7 | async-start | bytes 24576 | tf_op jit(solution)/shard_map/slice | solution.py:181
  55.4 54.5 %copy-start.17 = (pred[256,256]{0,1:T(8,128)(4,1)}, pred[256,256]{0,1:T(8,128)(4,1)S(1)}, u32[]{:S(2)}) copy-start(pred[256,256]{0,1:T(8,128)(4,1)S(1)} %fusion.84) | copy-start | bytes 196612
  94.9 4.9 copy-start.7
  95.1 4.7 copy-start.29
  102.9 7.1 %copy-start.9 = (bf16[256,1024]{0,1:T(8,128)(2,1)}, bf16[256,1024]{0,1:T(8,128)(2,1)S(1)}, u32[]{:S(2)}) copy-start(bf16[256,1024]{0,1:T(8,128)(2,1)S(1)} %copy.47) | copy-start | bytes 1572868
  107.1 2.9 copy-start.14
  109.1 2.2 copy-start.1
  110.0 3.1 slice-start.4
  110.0 1.6 copy-start.4
  110.0 4.7 slice-start.5
  111.2 1.8 copy-start.5
  111.3 3.4 slice-start.1
  112.3 5.1 slice-start.2
  112.8 4.6 copy-start.3
  114.7 2.7 slice-start.3
  117.4 2.9 copy-start.33
  117.4 4.3 copy-start.31
  117.4 13.2 %copy-start.32 = (s32[256]{0:T(256)S(1)}, s32[256]{0:T(256)}, u32[]{:S(2)}) copy-start(s32[256]{0:T(256)} %param.18) | copy-start | bytes 3076
  121.7 243.5 %reduce-scatter.8.cloned.1.call-start = ((), (), s32[]{:S(2)}) async-start(), calls=%async_computation.5 | async-start | bytes 9437184 | tf_op jit(solution)/shard_map/reduce_scatter | solution.py:247
  293.4 204.4 %reduce-scatter.10.cloned.1.call-start = ((), (), s32[]{:S(2)}) async-start(), calls=%async_computation.6 | async-start | bytes 14155776
  381.0 3.7 copy-start.6
  381.0 5.1 copy-start.13
  383.8 5.1 copy-start.18
  386.1 6.0 %copy-start.15 = (bf16[256,1024]{0,1:T(8,128)(2,1)S(1)}, bf16[256,1024]{0,1:T(8,128)(2,1)}, u32[]{:S(2)}) copy-start(bf16[256,1024]{0,1:T(8,128)(2,1)} %copy.45) | copy-start | bytes 1572868
  388.9 3.5 copy-start.2
  393.7 1.2 copy-start.11
  393.7 2.0 copy-start.10
  394.9 1.3 copy-start.20
  395.7 0.8 copy-start.30
  396.2 1.0 copy-start.16
  396.2 1.3 copy-start.8
  405.3 137.7 %copy-start.22 = (f32[1,3072]{1,0:T(1,128)S(1)}, f32[1,3072]{1,0:T(1,128)}, u32[]{:S(2)}) copy-start(f32[1,3072]{1,0:T(1,128)} %param.30) | copy-start | bytes 36868
  405.3 137.7 %copy-start.25 = (f32[1,3072]{1,0:T(1,128)S(1)}, f32[1,3072]{1,0:T(1,128)}, u32[]{:S(2)}) copy-start(f32[1,3072]{1,0:T(1,128)} %param.32) | copy-start | bytes 36868
  405.3 137.7 %copy-start.26 = (f32[1,3072]{1,0:T(1,128)S(1)}, f32[1,3072]{1,0:T(1,128)}, u32[]{:S(2)}) copy-start(f32[1,3072]{1,0:T(1,128)} %param.31) | copy-start | bytes 36868
Sparse Core Ops, SparseCore 0:
  39.6 51.2 reduce-scatter.5
  121.8 36.5 all-gather.4
  293.5 71.5 reduce-scatter.7
  405.4 92.2 reduce-scatter.9
where the time goes:
time: 557 us; the launch traced here: 553 us
  waiting for transfers between devices  219 us (39%)
  matrix products  130 us (23%)
  blocking collectives  103 us (18%)
  local copies, waits for them, and re-layouts  42.5 us (8%)
  other arithmetic  38.9 us (7%)
  between operations  19.2 us (3%)
    unnamed x5, waiting for transfers between devices  91.8 us
    reduce_scatter x1, waiting for transfers between devices, local(): lax.psum_scatter(mixed_product(grad_logits, embed_table), 'vocab', scatte...  71.7 us
    dot_general x9, matrix products, mixed_product(): return jnp.dot(left, right, preferred_element_type=jnp.float32)  65.3 us
    dot_general x1, matrix products, head_logits(): jnp.einsum('td,vd->tv', row_block, embed_table, preferred_element_type=jn...  35.7 us
    reduce_scatter x1, waiting for transfers between devices, local(): lax.psum_scatter(jnp.where(inside[:, None], picked_rows.astype(jnp.float3...  35.5 us
    psum x2, blocking collectives, local(): grad_shard, loss_sum = lax.psum((grad_shard, loss_part), 'dp')  27.7 us
    psum x2, blocking collectives, local(): row_total, picked = lax.psum((row_total, picked), 'vocab')  25.5 us
    reduce_sum x1, other arithmetic, local(): jnp.sum(jnp.where(columns[None, :] == wanted[:, None], logits, 0.0), -1)  20.5 us
  transfers between devices with their start and end apart: 4, of which 4 were waited for; matrix products, arithmetic and copies ran while one was open for 1% of the time, Pallas kernels for 0%

commit v1 on v0

--- a/solution.py
+++ b/solution.py
@@ -1,6 +1,11 @@
+import functools
+import math
+
 import jax
 import jax.numpy as jnp
 from jax import lax
+from jax.experimental import pallas as pl
+from jax.experimental.pallas import tpu as pltpu
 from jax.sharding import PartitionSpec as P
 
 MODEL_WIDTH = 1024
@@ -122,6 +127,456 @@
         axis=1,
     )
     return joined.astype(jnp.bfloat16)
+
+
+MESH = pl.DeviceIdType.MESH
+VMEM_CAP = 66 * 1000 * 1000
+NEG = -1e30
+
+
+def vspec():
+    return pl.BlockSpec(memory_space=pltpu.VMEM)
+
+
+def aspec():
+    return pl.BlockSpec(memory_space=pl.ANY)
+
+
+def xor_of(left, right, count):
+    total, bit = 0, 1
+    while bit < count:
+        total = total + ((left // bit + right // bit) % 2) * bit
+        bit *= 2
+    return total
+
+
+def greet(axis_counts):
+    barrier = pltpu.get_barrier_semaphore()
+    waits = 0
+    for axis, count in axis_counts:
+        me = lax.axis_index(axis)
+        for step in range(1, count):
+            pl.semaphore_signal(
+                barrier, inc=1, device_id={axis: lax.rem(me + step, count)}, device_id_type=MESH
+            )
+        waits += count - 1
+    pl.semaphore_wait(barrier, waits)
+
+
+def push(src, dst, send_sem, recv_sem, axis, peer):
+    return pltpu.make_async_remote_copy(
+        src_ref=src,
+        dst_ref=dst,
+        send_sem=send_sem,
+        recv_sem=recv_sem,
+        device_id={axis: peer},
+        device_id_type=MESH,
+    )
+
+
+def meta_kernel(n, ints_ref, adapt_ref, all_ints, all_adapt, send_sem, recv_sem):
+    me = lax.axis_index("vocab")
+    greet((("vocab", n),))
+    copies = []
+    for step in range(1, n):
+        peer = lax.rem(me + step, n)
+        for kind, (src, dst) in enumerate(((ints_ref, all_ints), (adapt_ref, all_adapt))):
+            copy = push(
+                src,
+                dst.at[me],
+                send_sem.at[kind, step],
+                recv_sem.at[kind, step],
+                "vocab",
+                peer,
+            )
+            copy.start()
+            copies.append(copy)
+    all_ints[me] = ints_ref[...]
+    all_adapt[me] = adapt_ref[...]
+    for copy in copies:
+        copy.wait()
+
+
+def gather_meta(n, ints, adapt):
+    return pl.pallas_call(
+        functools.partial(meta_kernel, n),
+        out_shape=(
+            jax.ShapeDtypeStruct((n,) + ints.shape, ints.dtype),
+            jax.ShapeDtypeStruct((n,) + adapt.shape, adapt.dtype),
+        ),
+        in_specs=[vspec(), vspec()],
+        out_specs=(vspec(), vspec()),
+        scratch_shapes=[pltpu.SemaphoreType.DMA((2, n)), pltpu.SemaphoreType.DMA((2, n))],
+        compiler_params=pltpu.CompilerParams(collective_id=1, has_side_effects=True),
+        name="gather_meta",
+    )(ints, adapt)
+
+
+def finish_kernel(
+    n, z, rows, total_tokens,
+    grads, adapt_ref, first_ref, second_ref, step_ref,
+    loss_out, norm_out, adapt_out, first_out, second_out, copy_out,
+    got_one, got_two, got_three, shard, squares, send_one, recv_one, send_two, recv_two, send_three, recv_three,
+):
+    me, mz = lax.axis_index("vocab"), lax.axis_index("dp")
+    greet((("vocab", n), ("dp", z)))
+    copies = []
+    for step in range(1, n):
+        peer = lax.rem(me + step, n)
+        copy = push(grads.at[peer], got_one.at[me], send_one.at[step], recv_one.at[step], "vocab", peer)
+        copy.start()
+        copies.append(copy)
+    got_one[me] = grads[me]
+    for copy in copies:
+        copy.wait()
+    total = got_one[0]
+    for source in range(1, n):
+        total = total + got_one[source]
+    shard[...] = total
+    copies = []
+    for step in range(1, z):
+        peer = lax.rem(mz + step, z)
+        copy = push(shard, got_two.at[mz], send_two.at[step], recv_two.at[step], "dp", peer)
+        copy.start()
+        copies.append(copy)
+    got_two[mz] = total
+    for copy in copies:
+        copy.wait()
+    total = got_two[0]
+    for source in range(1, z):
+        total = total + got_two[source]
+    shard[...] = total
+    grad = shard[:rows]
+    lanes = jnp.sum(grad * grad, axis=0, keepdims=True)
+    part = jnp.broadcast_to(lanes, squares.shape)
+    squares[...] = part
+    copies = []
+    for step in range(1, n):
+        peer = lax.rem(me + step, n)
+        copy = push(squares, got_three.at[me], send_three.at[step], recv_three.at[step], "vocab", peer)
+        copy.start()
+        copies.append(copy)
+    got_three[me] = part
+    for copy in copies:
+        copy.wait()
+    lanes = got_three[0]
+    for source in range(1, n):
+        lanes = lanes + got_three[source]
+    square_sum = jnp.sum(lanes[:1], axis=1, keepdims=True)
+    norm = jnp.sqrt(square_sum)
+    loss = jnp.sum(shard[rows : rows + 1], axis=1, keepdims=True) * (1.0 / total_tokens)
+    loss_out[...] = jnp.broadcast_to(loss, loss_out.shape)
+    norm_out[...] = jnp.broadcast_to(norm, norm_out.shape)
+    clipped = grad * jnp.minimum(1.0, CLIP_NORM / (norm + 1e-06))
+    count = jnp.full((1, 128), step_ref[0], jnp.int32).astype(jnp.float32)
+    fix_one = 1.0 - jnp.exp(count * math.log(BETA_ONE))
+    fix_two = 1.0 - jnp.exp(count * math.log(BETA_TWO))
+    new_first = BETA_ONE * first_ref[...] + (1.0 - BETA_ONE) * clipped
+    new_second = BETA_TWO * second_ref[...] + (1.0 - BETA_TWO) * clipped * clipped
+    master = adapt_ref[...]
+    motion = (
+        new_first / fix_one / (jnp.sqrt(new_second / fix_two) + ADAM_EPS) + WEIGHT_DECAY * master
+    )
+    new_master = master - LEARN_RATE * motion
+    adapt_out[...] = new_master
+    first_out[...] = new_first
+    second_out[...] = new_second
+    copy_out[...] = new_master.astype(jnp.bfloat16)
+
+
+def finish(n, z, total_tokens, grads, adapters, first, second, step):
+    rows, block = adapters.shape[0], grads.shape[1]
+    f32 = jnp.float32
+    flat = jax.ShapeDtypeStruct((rows, 128), f32)
+    tile = jax.ShapeDtypeStruct((8, 128), f32)
+    dma = pltpu.SemaphoreType.DMA
+    return pl.pallas_call(
+        functools.partial(finish_kernel, n, z, rows, total_tokens),
+        out_shape=(tile, tile, flat, flat, flat, jax.ShapeDtypeStruct((rows, 128), jnp.bfloat16)),
+        in_specs=[vspec()] * 4 + [pl.BlockSpec(memory_space=pltpu.SMEM)],
+        out_specs=(vspec(),) * 6,
+        scratch_shapes=[
+            pltpu.VMEM((n, block, 128), f32),
+            pltpu.VMEM((z, block, 128), f32),
+            pltpu.VMEM((n, 8, 128), f32),
+            pltpu.VMEM((block, 128), f32),
+            pltpu.VMEM((8, 128), f32),
+            dma((n,)), dma((n,)), dma((z,)), dma((z,)), dma((n,)), dma((n,)),
+        ],
+        compiler_params=pltpu.CompilerParams(collective_id=2, has_side_effects=True),
+        name="finish",
+    )(grads, adapters, first, second, step)
+
+
+def head_kernel(
+    n, rows, padded, chunk, vocab_real,
+    hid_ref, targets_ref, weights_ref, table_ref,
+    dhid_out, loss_out,
+    table, probs, hid_all, logit_a, logit_b, tops, run_top, run_sum, run_pick, columns,
+    stats, got_stats, lse_cols, dl_a, dl_b, partial, sib_send, off_send,
+    load_sem, own_sem, hid_send, hid_recv, fwd_send, stat_send, stat_recv, sib_sem, sib_recv, off_sem, off_recv,
+):
+    f32, bf16 = jnp.float32, jnp.bfloat16
+    tokens, width = hid_ref.shape
+    pairs, chunks, ring = n // 2, padded // chunk, off_send.shape[0]
+    me = lax.axis_index("vocab")
+    sibling = xor_of(me, 1, n)
+    held = table_ref.shape[0]
+    load = pltpu.make_async_copy(table_ref, table.at[pl.ds(0, held)], load_sem)
+    load.start()
+    own = pltpu.make_async_copy(hid_ref, hid_all.at[0], own_sem)
+    own.start()
+    if padded > held:
+        table[held:] = jnp.zeros((padded - held, width), bf16)
+    greet((("vocab", n),))
+
+    for slot in (1,) + tuple(range(2, n, 2)):
+        push(hid_ref, hid_all.at[slot], hid_send.at[slot], hid_recv.at[slot], "vocab", xor_of(me, slot, n)).start()
+
+    lane = lax.broadcasted_iota(jnp.int32, (tokens, 128), 1)
+    flane = lane.astype(f32)
+    step_rows = 32
+    small_lane = lax.broadcasted_iota(jnp.int32, (step_rows, 128), 1).astype(f32)
+
+    base = (me * rows).astype(f32)
+    pad_rows = 128 - n
+    goals = targets_ref[...] - base
+    goals = jnp.where(jnp.logical_and(goals >= 0.0, goals < float(rows)), goals, -1.0)
+    columns[...] = jnp.concatenate([goals, jnp.zeros((pad_rows, tokens), f32)], axis=0).T
+
+    def column_of(array, index):
+        return jnp.sum(jnp.where(lane == index, array, 0.0), axis=1, keepdims=True)
+
+    stats[...] = jnp.zeros(stats.shape, f32)
+    live = jnp.minimum(rows, vocab_real - me * rows).astype(f32)
+    dead_from = rows - (rows * n - vocab_real)
+
+    def soft_chunk(slot, index, logit, target):
+        for first in range(0, tokens, step_rows):
+            part = slice(first, first + step_rows)
+            old = run_top[part]
+            top = old
+            ragged = (index + 1) * chunk > dead_from
+            for q in range(0, chunk, 128):
+                if ragged and index * chunk + q + 128 > dead_from:
+                    kept = jnp.where(small_lane + float(index * chunk + q) < live, logit[part, q : q + 128], NEG)
+                    logit[part, q : q + 128] = kept
+                    top = jnp.maximum(top, kept)
+                else:
+                    top = jnp.maximum(top, logit[part, q : q + 128])
+            total = run_sum[part] * jnp.exp(old - top)
+            pick = run_pick[part]
+            goal = target[part]
+            for q in range(0, chunk, 128):
+                value = logit[part, q : q + 128]
+                grown = jnp.exp(value - top)
+                total = total + grown
+                pick = jnp.where(small_lane + float(index * chunk + q) == goal, value, pick)
+                probs[slot, part, index * chunk + q : index * chunk + q + 128] = grown.astype(bf16)
+            tops[slot, index, part] = top
+            run_top[part] = top
+            run_sum[part] = total
+            run_pick[part] = pick
+
+    def first_pass(slot, _):
+        even = lax.rem(slot, 2) == 0
+
+        @pl.when(slot > 0)
+        def _():
+            push(hid_ref, hid_all.at[slot], hid_send.at[slot], hid_recv.at[slot], "vocab", sibling).wait_recv()
+
+        @pl.when(jnp.logical_and(slot > 0, even))
+        def _():
+            push(
+                hid_all.at[slot], hid_all.at[slot + 1], fwd_send.at[slot], hid_recv.at[slot + 1], "vocab", sibling
+            ).start()
+
+        block = xor_of(me, slot, n)
+        target = jnp.broadcast_to(column_of(columns[...], block), (tokens, 128))
+        run_top[...] = jnp.full((tokens, 128), NEG, f32)
+        run_sum[...] = jnp.zeros((tokens, 128), f32)
+        run_pick[...] = jnp.zeros((tokens, 128), f32)
+        logit = (logit_a, logit_b)
+        for index in range(chunks):
+            logit[index % 2][...] = lax.dot_general(
+                hid_all[slot],
+                table[index * chunk : (index + 1) * chunk],
+                (((1,), (1,)), ((), ())),
+                preferred_element_type=f32,
+            )
+            if index > 0:
+                soft_chunk(slot, index - 1, logit[(index - 1) % 2], target)
+        soft_chunk(slot, chunks - 1, logit[(chunks - 1) % 2], target)
+        lane_top = run_top[...]
+        top = jnp.max(lane_top, axis=1, keepdims=True)
+        total = jnp.sum(run_sum[...] * jnp.exp(lane_top - top), axis=1, keepdims=True)
+        pick = jnp.sum(run_pick[...], axis=1, keepdims=True)
+        stats[...] = jnp.where(
+            lane == block,
+            top,
+            jnp.where(lane == block + n, total, jnp.where(lane == block + 2 * n, pick, stats[...])),
+        )
+        return 0
+
+    own.wait()
+    load.wait()
+    lax.fori_loop(0, n, first_pass, 0)
+
+    for slot in (1,) + tuple(range(2, n, 2)):
+        push(hid_ref, hid_all.at[slot], hid_send.at[slot], hid_recv.at[slot], "vocab", sibling).wait_send()
+    for slot in range(2, n, 2):
+        push(hid_all.at[slot], hid_all.at[slot + 1], fwd_send.at[slot], hid_recv.at[slot + 1], "vocab", sibling).wait_send()
+
+    got_stats[0] = stats[...].T[: 3 * n]
+    copies = []
+    for slot in range(1, n):
+        copy = push(
+            got_stats.at[0], got_stats.at[slot], stat_send.at[slot], stat_recv.at[slot], "vocab", xor_of(me, slot, n)
+        )
+        copy.start()
+        copies.append(copy)
+    for copy in copies:
+        copy.wait()
+    top = got_stats[0, :n]
+    for slot in range(1, n):
+        top = jnp.maximum(top, got_stats[slot, :n])
+    total = jnp.zeros((n, tokens), f32)
+    pick = jnp.zeros((n, tokens), f32)
+    for slot in range(n):
+        total = total + got_stats[slot, n : 2 * n] * jnp.exp(got_stats[slot, :n] - top)
+        pick = pick + got_stats[slot, 2 * n : 3 * n]
+    row_lse = top + jnp.log(total)
+    weights = weights_ref[...]
+    mine = lax.broadcasted_iota(jnp.int32, (n, tokens), 0) == me
+    loss_row = jnp.sum(jnp.where(mine, weights * (row_lse - pick), 0.0), axis=0, keepdims=True)
+    loss_lanes = loss_row[:, :128]
+    for q in range(128, tokens, 128):
+        loss_lanes = loss_lanes + loss_row[:, q : q + 128]
+    loss_out[...] = jnp.broadcast_to(loss_lanes, loss_out.shape)
+    spare = 128 - 2 * n
+    lse_cols[...] = jnp.concatenate([row_lse, weights, jnp.zeros((spare, tokens), f32)], axis=0).T
+
+    def scale_block(slot, out):
+        block = xor_of(me, slot, n)
+        goal_all = jnp.broadcast_to(column_of(columns[...], block), (tokens, 128))
+        lse_all = jnp.broadcast_to(column_of(lse_cols[...], block), (tokens, 128))
+        weight_all = jnp.broadcast_to(column_of(lse_cols[...], block + n), (tokens, 128))
+        for first in range(0, tokens, step_rows):
+            part = slice(first, first + step_rows)
+            goal, weight, lse = goal_all[part], weight_all[part], lse_all[part]
+            for index in range(chunks):
+                factor = weight * jnp.exp(tops[slot, index, part] - lse)
+                for q in range(index * chunk, (index + 1) * chunk, 128):
+                    hit = jnp.where(small_lane + float(q) == goal, weight, 0.0)
+                    grown = probs[slot, part, q : q + 128].astype(f32)
+                    out[part, q : q + 128] = (grown * factor - hit).astype(bf16)
+
+    def sib_copy(pair):
+        return push(
+            sib_send.at[lax.rem(pair, 2)],
+            hid_all.at[2 * pair],
+            sib_sem.at[pair],
+            sib_recv.at[pair],
+            "vocab",
+            sibling,
+        )
+
+    def off_copy(pair):
+        return push(
+            off_send.at[lax.rem(pair, ring)],
+            hid_all.at[2 * pair + 1],
+            off_sem.at[pair],
+            off_recv.at[pair],
+            "vocab",
+            xor_of(me, 2 * pair, n),
+        )
+
+    scale_block(n - 1, dl_a)
+
+    def second_pass(trip, _):
+        pair = pairs - 1 - trip
+
+        @pl.when(trip > 1)
+        def _():
+            sib_copy(pair + 2).wait_send()
+
+        scale_block(2 * pair, dl_b)
+        sib_send[lax.rem(pair, 2)] = jnp.dot(dl_a[...], table[...], preferred_element_type=f32).astype(bf16)
+        sib_copy(pair).start()
+
+        scale_block(jnp.maximum(2 * pair - 1, 0), dl_a)
+        partial[...] = jnp.dot(dl_b[...], table[...], preferred_element_type=f32)
+        sib_copy(pair).wait_recv()
+
+        @pl.when(pair > 0)
+        def _():
+            @pl.when(trip >= ring)
+            def _():
+                off_copy(pair + ring).wait_send()
+
+            off_send[lax.rem(pair, ring)] = (partial[...] + hid_all[2 * pair].astype(f32)).astype(bf16)
+            off_copy(pair).start()
+
+        return 0
+
+    lax.fori_loop(0, pairs, second_pass, 0)
+    for pair in range(min(2, pairs)):
+        sib_copy(pair).wait_send()
+    for pair in range(1, pairs):
+        if pair <= ring:
+            off_copy(pair).wait_send()
+        off_copy(pair).wait_recv()
+    total = partial[...] + hid_all[0].astype(f32)
+    for pair in range(1, pairs):
+        total = total + hid_all[2 * pair + 1].astype(f32)
+    dhid_out[...] = total
+
+
+def head(n, hid, targets, weights, table):
+    tokens, width = hid.shape
+    rows = table.shape[0]
+    padded = -(-rows // 128) * 128
+    if rows % 16:
+        table = jnp.pad(table, ((0, padded - rows), (0, 0)))
+    groups = padded // 128
+    per = max(part for part in range(1, 14) if groups % part == 0)
+    chunk = per * 128
+    f32, bf16 = jnp.float32, jnp.bfloat16
+    dma = pltpu.SemaphoreType.DMA
+    pairs = n // 2
+    ring = max(1, min(pairs - 1, 3))
+    return pl.pallas_call(
+        functools.partial(head_kernel, n, rows, padded, chunk, VOCAB_REAL),
+        out_shape=(jax.ShapeDtypeStruct((tokens, width), f32), jax.ShapeDtypeStruct((8, 128), f32)),
+        in_specs=[vspec(), vspec(), vspec(), aspec()],
+        out_specs=(vspec(), vspec()),
+        scratch_shapes=[
+            pltpu.VMEM((padded, width), bf16),
+            pltpu.VMEM((n, tokens, padded), bf16),
+            pltpu.VMEM((n, tokens, width), bf16),
+            pltpu.VMEM((tokens, chunk), f32),
+            pltpu.VMEM((tokens, chunk), f32),
+            pltpu.VMEM((n, padded // chunk, tokens, 128), f32),
+            pltpu.VMEM((tokens, 128), f32),
+            pltpu.VMEM((tokens, 128), f32),
+            pltpu.VMEM((tokens, 128), f32),
+            pltpu.VMEM((tokens, 128), f32),
+            pltpu.VMEM((tokens, 128), f32),
+            pltpu.VMEM((n, 3 * n, tokens), f32),
+            pltpu.VMEM((tokens, 128), f32),
+            pltpu.VMEM((tokens, padded), bf16),
+            pltpu.VMEM((tokens, padded), bf16),
+            pltpu.VMEM((tokens, width), f32),
+            pltpu.VMEM((2, tokens, width), bf16),
+            pltpu.VMEM((ring, tokens, width), bf16),
+            dma, dma, dma((n,)), dma((n,)), dma((n,)), dma((n,)), dma((n,)),
+            dma((pairs,)), dma((pairs,)), dma((pairs,)), dma((pairs,)),
+        ],
+        compiler_params=pltpu.CompilerParams(
+            collective_id=3, has_side_effects=True, vmem_limit_bytes=VMEM_CAP
+        ),
+        name="head",
+    )(hid, targets, weights, table)
 
 
 def local(
@@ -147,12 +602,14 @@
     vocab_count = lax.axis_size("vocab")
     total_tokens = TOK_DEV * vocab_count * lax.axis_size("dp")
     shard_rows = embed_table.shape[0]
-    all_tokens, all_targets, all_mask = (
-        lax.all_gather(token_ids, "vocab", axis=0, tiled=True),
-        lax.all_gather(target_ids, "vocab", axis=0, tiled=True),
-        lax.all_gather(loss_mask, "vocab", axis=0, tiled=True),
-    )
-    mask_weights = all_mask.astype(jnp.float32)
+    zero_row = jnp.zeros_like(token_ids)
+    ints, adapter_parts = gather_meta(
+        vocab_count,
+        jnp.stack([token_ids, target_ids, loss_mask] + [zero_row] * 5),
+        adapters.astype(jnp.bfloat16).reshape(-1, 128),
+    )
+    all_tokens = ints[:, 0].reshape(-1)
+    copies = adapter_parts.reshape(1, -1)
     wanted = all_tokens - vocab_place * shard_rows
     inside = (wanted >= 0) & (wanted < shard_rows)
     picked_rows = jnp.take(embed_table, jnp.clip(wanted, 0, shard_rows - 1), axis=0)
@@ -162,7 +619,6 @@
         scatter_dimension=0,
         tiled=True,
     ).astype(jnp.float32)
-    copies = lax.all_gather(adapters.astype(jnp.bfloat16), "vocab", axis=1, tiled=True)
     resid = embedded + pos_table[positions_of(seq_ids)].astype(jnp.float32)
     place = jnp.arange(TOK_DEV)
     visible = (seq_ids[:, None] == seq_ids[None, :]) & (place[None, :] <= place[:, None])
@@ -218,34 +674,12 @@
     ]
     hidden, normed_last, inverse_last = layer_norm(resid, gains[2 * LAYERS], shifts[2 * LAYERS])
     hidden = hidden.astype(jnp.bfloat16)
-    columns = vocab_place * shard_rows + jnp.arange(shard_rows)
-    live = columns < VOCAB_REAL
-
-    def head_logits(row_block):
-        logits = jnp.einsum("td,vd->tv", row_block, embed_table, preferred_element_type=jnp.float32)
-        return jnp.where(live[None], logits, -1e30)
-
-    piece = lax.all_gather(hidden, "vocab", axis=0, tiled=True)
-    logits = head_logits(piece)
-    row_top = jnp.max(logits, -1)
-    row_total = jnp.sum(jnp.exp(logits - row_top[:, None]), -1)
-    wanted = all_targets
-    picked = jnp.sum(jnp.where(columns[None, :] == wanted[:, None], logits, 0.0), -1)
-    gathered, row_top, row_total, picked = (piece, row_top, row_total, picked)
-    joint_top = lax.pmax(row_top, "vocab")
-    row_total = row_total * jnp.exp(row_top - joint_top)
-    row_total, picked = lax.psum((row_total, picked), "vocab")
-    row_lse = joint_top + jnp.log(row_total)
-    loss_part = jnp.sum(mask_weights * (row_lse - picked))
-    row_block = gathered
-    logits = head_logits(row_block)
-    wanted = all_targets
-    hit = (columns[None, :] == wanted[:, None]).astype(jnp.float32)
-    grad_logits = (
-        mask_weights[:, None] * (jnp.exp(logits - row_lse[:, None]) - hit) * (1.0 / total_tokens)
-    ).astype(jnp.bfloat16)
-    grad_hidden = lax.psum_scatter(
-        mixed_product(grad_logits, embed_table), "vocab", scatter_dimension=0, tiled=True
+    grad_hidden, loss_rows = head(
+        vocab_count,
+        hidden,
+        ints[:, 1].astype(jnp.float32),
+        ints[:, 2].astype(jnp.float32) * (1.0 / total_tokens),
+        embed_table,
     )
     grad_resid = norm_back(grad_hidden, normed_last, inverse_last, gains[2 * LAYERS])
     layer_grads = []
@@ -312,23 +746,31 @@
                 ]
             ),
         )
-    local_grads = jnp.stack(layer_grads)
-    grad_shard = lax.psum_scatter(local_grads, "vocab", scatter_dimension=1, tiled=True)
-    grad_shard, loss_sum = lax.psum((grad_shard, loss_part), "dp")
-    square_sum = lax.psum(jnp.sum(grad_shard * grad_shard), "vocab")
-    loss = loss_sum / total_tokens
-    grad_norm = jnp.sqrt(square_sum)
-    clipped = grad_shard * jnp.minimum(1.0, CLIP_NORM / (grad_norm + 1e-06))
-    step = step_count[0].astype(jnp.float32)
-    new_first = BETA_ONE * first_moment + (1.0 - BETA_ONE) * clipped
-    new_second = BETA_TWO * second_moment + (1.0 - BETA_TWO) * clipped * clipped
-    fix_one = 1.0 - jnp.power(BETA_ONE, step)
-    fix_two = 1.0 - jnp.power(BETA_TWO, step)
-    motion = (
-        new_first / fix_one / (jnp.sqrt(new_second / fix_two) + ADAM_EPS) + WEIGHT_DECAY * adapters
-    )
-    new_adapters = adapters - LEARN_RATE * motion
-    return (loss, grad_norm, new_adapters, new_first, new_second, new_adapters.astype(jnp.bfloat16))
+    flat = layer_grads[0].reshape(vocab_count, -1, 128)
+    shard_lines = flat.shape[1]
+    spare = -(shard_lines + 1) % 8
+    loss_line = jnp.broadcast_to(loss_rows[:1][None], (vocab_count, 1, 128))
+    grads = jnp.concatenate(
+        [flat, loss_line, jnp.zeros((vocab_count, spare, 128), jnp.float32)], axis=1
+    )
+    loss, grad_norm, new_adapters, new_first, new_second, rounded = finish(
+        vocab_count,
+        lax.axis_size("dp"),
+        1.0,
+        grads,
+        adapters.reshape(-1, 128),
+        first_moment.reshape(-1, 128),
+        second_moment.reshape(-1, 128),
+        step_count,
+    )
+    return (
+        loss[0, 0],
+        grad_norm[0, 0],
+        new_adapters.reshape(1, -1),
+        new_first.reshape(1, -1),
+        new_second.reshape(1, -1),
+        rounded.reshape(1, -1),
+    )
 
 
 def solution(mesh):

time: 557 us -> 287 us (0.52)
  waiting for transfers between devices: 219 us -> 42.9 us
  Pallas kernels: 0 us -> 122 us
  blocking collectives: 103 us -> 0 us
  matrix products: 130 us -> 43.1 us
  other arithmetic: 38.9 us -> 21.8 us
  local copies, waits for them, and re-layouts: 42.5 us -> 36.5 us
    pallas_call x0 -> x3, Pallas kernels: none -> 122 us  [the longest x1 98.9 us: head(): pl.pallas_call(functools.partial(head_kernel, n, rows, padded, chunk, VOC...]
    unnamed x5 -> x1, waiting for transfers between devices: 91.8 us -> 0.02 us
    reduce_scatter x1 -> x0, waiting for transfers between devices: 71.7 us -> none  [local(): lax.psum_scatter(mixed_product(grad_logits, embed_table), 'vocab', scatte...]
    psum x4 -> x0, blocking collectives: 53.2 us -> none  [the longest x2 27.7 us: local(): grad_shard, loss_sum = lax.psum((grad_shard, loss_part), 'dp')]
    dot_general x9 -> x8, matrix products: 65.3 us -> 15.5 us  [mixed_product(): return jnp.dot(left, right, preferred_element_type=jnp.float32)]
    all_gather x4 -> x0, blocking collectives: 37 us -> none  [the longest x1 10.7 us: local(): lax.all_gather(token_ids, 'vocab', axis=0, tiled=True)]
    dot_general x2 -> x1, matrix products: 37.6 us -> 0.83 us  [attention_back(): jnp.einsum('qhd,khd->hqk', query, keys, preferred_element_type=jnp.float32)]
    reduce_sum x3 -> x0, other arithmetic: 21.7 us -> none  [the longest x1 20.5 us: local(): jnp.sum(jnp.where(columns[None, :] == wanted[:, None], logits, 0.0), -1)]
  transfers between devices with their start and end apart: 4 -> 1, of which waited for: 4 -> 1; matrix products, arithmetic and copies ran while one was open for 1% -> 3% of each run, Pallas kernels for 0% -> 0%
where the time goes in v1:
time: 287 us; the launch traced here: 282 us
  Pallas kernels  122 us (43%)
  matrix products  43.1 us (15%)
  waiting for transfers between devices  42.9 us (15%)
  local copies, waits for them, and re-layouts  36.5 us (13%)
  other arithmetic  21.8 us (8%)
  between operations  15.7 us (5%)
    pallas_call x1, Pallas kernels, head(): pl.pallas_call(functools.partial(head_kernel, n, rows, padded, chunk, VOC...  98.9 us
    reduce_scatter x1, waiting for transfers between devices, local(): lax.psum_scatter(jnp.where(inside[:, None], picked_rows.astype(jnp.float3...  42.9 us
    gather x1, local copies, waits for them, and re-layouts, local(): jnp.take(embed_table, jnp.clip(wanted, 0, shard_rows - 1), axis=0)  17.3 us
    dot_general x8, matrix products, mixed_product(): return jnp.dot(left, right, preferred_element_type=jnp.float32)  15.5 us
    pallas_call x1, Pallas kernels, finish(): pl.pallas_call(functools.partial(finish_kernel, n, z, rows, total_tokens)...  15.3 us
    dot_general x1, matrix products, local(): jnp.einsum('tf,df->td', grad_pre, w_fc[layer_params], preferred_element_t...  14.7 us
    pallas_call x1, Pallas kernels, gather_meta(): pl.pallas_call(functools.partial(meta_kernel, n), out_shape=(jax.ShapeDty...  8.18 us
    unnamed x64, local copies, waits for them, and re-layouts  7.13 us
  transfers between devices with their start and end apart: 1, of which 1 were waited for; matrix products, arithmetic and copies ran while one was open for 3% of the time, Pallas kernels for 0%

profile of v1, /device:TPU:0, one launch (start us, length us, event | category | flops | bytes accessed | tf_op | source)
XLA Modules:
  0.0 282.5 jit_solution(8021214137491685115)
XLA Ops:
  7.2 1.3 convert_reduce_fusion
  8.6 1.3 stack.19.ints_ref
  9.9 8.2 %gather_meta.1 = (s32[8,8,256]{2,1,0:T(8,128)}, bf16[8,24,128]{2,1,0:T(8,128)(2,1)}) custom-call(s32[8,256]{1,0:T(8,128)} %stack.19.ints_ref, bf16[24,128]{1,0:T(8,128)(2,1)} %bitcast.168), custom_call_target="tpu_custom_call" | custom-call | tf_op jit(solution)/shard_map/gather_meta/pallas_call | solution.py:201
  18.1 0.9 and_reduce_fusion
  18.9 0.9 broadcast_clamp_fusion.1
  19.9 17.3 %gather_fusion = bf16[2048,1024]{1,0:T(8,128)(2,1)} fusion(bf16[6288,1024]{1,0:T(8,128)(2,1)} %table_ref.1, s32[2048]{0:T(1024)S(1)} %broadcast_clamp_fusion), kind=kCustom, calls=%fused_computation | custom fusion | bytes 8396800 | tf_op jit(solution)/shard_map/jit(_take)/gather | solution.py:615
  37.2 4.4 %select_convert_fusion = bf16[2048,1024]{1,0:T(8,128)(2,1)} fusion(bf16[2048,1024]{1,0:T(8,128)(2,1)} %gather_fusion, pred[2048]{0:T(1024)(128)(4,1)S(1)} %compare_and_fusion, pred[2048]{0:T(1024)(128)(4,1)S(1)} %and.26), kind=kLoop, calls=%fused_computation.10 | loop fusion | flops 8388608 | bytes 8392704 | tf_op jit(solution)/shard_map/convert_element_type | solution.py:617
  41.7 0.7 copy-done.19
  42.5 4.6 %slice.109 = bf16[6144,4]{1,0:T(8,128)(2,1)} reshape(bf16[8,24,128]{2,1,0:T(8,128)(2,1)S(1)} %copy-done.18) | data formatting | bytes 98304 | tf_op jit(solution)/shard_map/slice | solution.py:73
  48.6 1.2 gather_fusion.1
  49.8 0.6 fusion.82.weights_ref
  50.4 0.6 fusion.83.targets_ref
  51.2 42.9 %reduce-scatter.2.cloned.1.call-done = bf16[256,1024]{1,0:T(8,128)(2,1)} async-done(((bf16[2048,1024]{1,0:T(8,128)(2,1)}), bf16[256,1024]{1,0:T(8,128)(2,1)}) %reduce-scatter.2.cloned.1.call-update) | async-done | bytes 524304 | tf_op jit(solution)/shard_map/reduce_scatter | solution.py:616
  94.1 1.3 fusion.70
  95.4 1.3 multiply_reduce_fusion.5
  96.7 1.3 add_convert_fusion.3
  98.0 1.4 convolution_convert_fusion.1
  99.4 4.6 %fusion.20 = f32[256,3072]{1,0:T(8,128)S(1)} fusion(bf16[256,1024]{1,0:T(8,128)(2,1)S(1)} %add_convert_fusion.3, bf16[1,1024,3072]{2,1,0:T(8,128)(2,1)} %param.26, f32[3072]{0:T(1024)S(1)} %bitcast.165), kind=kOutput, calls=%fused_computation.33 | convolution fusion | flops 1611399168 | bytes 9973760 | tf_op jit(solution)/shard_map/dot_general | solution.py:32
  104.1 0.6 fusion.23
  105.5 0.8 select_reduce_fusion
  106.3 0.9 fusion.26
  107.3 1.2 fusion.64
  108.6 1.9 convolution_convert_fusion
  110.5 0.7 fusion.47
  112.1 3.0 %fusion.10 = f32[256,4096]{1,0:T(8,128)S(1)} fusion(bf16[1,1024,4096]{2,1,0:T(8,128)(2,1)S(1)} %bitcast.191, f32[4096]{0:T(1024)S(1)} %bitcast.166, f32[256,1024]{1,0:T(8,128)S(1)} %get-tuple-element.44, f32[1024]{0:T(1024)S(1)} %bitcast.184, f32[1024]{0:T(1024)S(1)} %bitcast.181, f32[256]{0:T(256)S(1)} %add_rsqrt_fusion.1, f32[256]{0:T(256)S(1)} %broadcast_multiply_fusion.5), kind=kOutput, calls=%fused_computation.17 | convolution fusion | flops 2149842944 | bytes 13658112 | tf_op jit(solution)/shard_map/dot_general | solution.py:32
  115.2 2.8 %fusion.107 = (f32[256]{0:T(256)S(1)}, f32[256,1024]{1,0:T(8,128)S(1)}) fusion(f32[1024]{0:T(1024)S(1)} %bitcast.183, f32[256,1024]{1,0:T(8,128)S(1)} %get-tuple-element.44, bf16[1,4096,1024]{2,1,0:T(8,128)(2,1)S(1)} %bitcast.189, f32[256,4096]{1,0:T(8,128)S(1)} %fusion.10), kind=kOutput, calls=%fused_computation.158 | convolution fusion | flops 2157707008 | bytes 14685184 | tf_op jit(solution)/shard_map/dot_general | solution.py:32
  118.3 0.7 copy-done.2
  119.0 1.1 add_convert_fusion.1.hid_ref
  120.1 98.9 %head.1 = (f32[256,1024]{1,0:T(8,128)}, f32[8,128]{1,0:T(8,128)}) custom-call(bf16[256,1024]{1,0:T(8,128)(2,1)} %add_convert_fusion.1.hid_ref, f32[8,256]{1,0:T(8,128)} %fusion.83.targets_ref, f32[8,256]{1,0:T(8,128)} %fusion.82.weights_ref, bf16[6288,1024]{1,0:T(8,128)(2,1)} %table_ref.1), custom_call_target="tpu_custom_call" | custom-call | tf_op jit(solution)/shard_map/head/pallas_call | solution.py:548
  219.1 1.9 multiply_reduce_fusion.6
  220.9 14.7 %fusion.101 = (f32[256]{0:T(256)S(1)}, f32[256]{0:T(256)S(1)}, f32[256,1024]{1,0:T(8,128)}) fusion(f32[256]{0:T(256)S(1)} %add_rsqrt_fusion.1, f32[256,1024]{1,0:T(8,128)} %copy-done.4, f32[256]{0:T(256)S(1)} %broadcast_multiply_fusion.5, f32[1024]{0:T(1024)S(1)} %bitcast.182, bf16[1,1024,4096]{2,1,0:T(8,128)(2,1)} %param.28, f32[256,4096]{1,0:T(8,128)} %copy-done.24, ...), kind=kOutput, calls=%fused_computation.152 | convolution fusion | flops 4323803136 | bytes 25182208 | tf_op jit(solution)/shard_map/tf,df->td/dot_general | solution.py:708
  235.7 2.3 add_convert_fusion
  238.4 0.8 fusion.30
  239.8 1.7 fusion.61
  241.7 3.2 %fusion.65 = bf16[16,64,256]{2,1,0:T(8,128)(2,1)S(1)} fusion(bf16[256,16,64]{0,2,1:T(8,128)(2,1)S(1)} %bitcast.147, f32[16,256,256]{1,2,0:T(8,128)} %copy-done, f32[16,256]{1,0:T(8,128)S(1)} %log_add_fusion, pred[256,256]{0,1:T(8,128)(4,1)S(1)} %fusion.78), kind=kOutput, calls=%fused_computation.67 | convolution fusion | flops 138674176 | bytes 5324800 | tf_op jit(solution)/shard_map/hqk,qhd->khd/dot_general | solution.py:110
  245.1 1.4 multiply_reduce_fusion
  246.5 1.2 multiply_convert_fusion
  247.7 0.8 fusion.63
  249.8 0.7 slice_bitcast_fusion
  250.8 0.7 fusion.112
  251.8 0.7 maximum_maximum_fusion.grads
  252.5 15.3 %finish.1 = (f32[8,128]{1,0:T(8,128)}, f32[8,128]{1,0:T(8,128)}, f32[24,128]{1,0:T(8,128)}, f32[24,128]{1,0:T(8,128)}, f32[24,128]{1,0:T(8,128)}, /*index=5*/bf16[24,128]{1,0:T(8,128)(2,1)}) custom-call(f32[8,32,128]{2,1,0:T(8,128)} %maximum_maximum_fusion.grads, f32[24,128]{1,0:T(8,128)} %bitcast.163, f32[24,128]{1,0:T(8,128)} %bitcast.176, ...), custom_call_target="tpu_custom_call" | custom-call | tf_op jit(solution)/shard_map/finish/pallas_call | solution.py:293
  267.8 1.2 slice.129
  269.0 1.2 slice.128
  270.2 1.3 copy.61
  271.5 1.3 copy.66
  272.8 1.3 copy.67
  274.1 1.3 copy.68
  (119 shorter events, 6.4 us)
Async XLA Ops:
  7.2 86.9 %reduce-scatter.2.cloned.1.call-start = ((), (), s32[]{:S(2)}) async-start(), calls=%async_computation.1 | async-start | bytes 4718592 | tf_op jit(solution)/shard_map/reduce_scatter | solution.py:616
  41.6 0.8 copy-start.19
  41.6 0.9 copy-start.18
  41.6 6.1 %copy-start.21 = (s32[256]{0:T(256)S(1)}, s32[256]{0:T(256)}, u32[]{:S(2)}) copy-start(s32[256]{0:T(256)} %param.20) | copy-start | bytes 3076
  41.6 7.0 %copy-start.6 = (bf16[1024,1024]{1,0:T(8,128)(2,1)S(1)}, bf16[1024,1024]{1,0:T(8,128)(2,1)}, u32[]{:S(2)}) copy-start(bf16[1024,1024]{1,0:T(8,128)(2,1)} %param.22) | copy-start | bytes 6291460
  41.6 8.2 %copy-start.20 = (f32[1,9216]{1,0:T(1,128)S(1)}, f32[1,9216]{1,0:T(1,128)}, u32[]{:S(2)}) copy-start(f32[1,9216]{1,0:T(1,128)} %param.25) | copy-start | bytes 110596
  41.6 9.4 %copy-start.22 = (f32[3,1024]{1,0:T(4,128)S(1)}, f32[3,1024]{1,0:T(4,128)}, u32[]{:S(2)}) copy-start(f32[3,1024]{1,0:T(4,128)} %param.23) | copy-start | bytes 36868
  41.6 9.4 %copy-start.23 = (f32[3,1024]{1,0:T(4,128)S(1)}, f32[3,1024]{1,0:T(4,128)}, u32[]{:S(2)}) copy-start(f32[3,1024]{1,0:T(4,128)} %param.24) | copy-start | bytes 36868
  48.6 50.8 %slice-start = ((f32[1,9216]{1,0:T(1,128)}), f32[1,3072]{1,0:T(1,128)S(1)}, s32[]{:S(2)}) async-start(f32[1,9216]{1,0:T(1,128)} %param.25), calls=%async_computation.2 | async-start | bytes 24576 | tf_op jit(solution)/shard_map/slice | solution.py:637
  98.0 6.0 %copy-start.10 = (bf16[256,1024]{1,0:T(8,128)(2,1)}, bf16[256,1024]{1,0:T(8,128)(2,1)S(1)}, u32[]{:S(2)}) copy-start(bf16[256,1024]{1,0:T(8,128)(2,1)S(1)} %add_convert_fusion.3) | copy-start | bytes 1572868
  105.1 2.2 copy-start.12
  105.3 2.0 copy-start.16
  105.5 1.7 copy-start.14
  106.3 2.2 copy-start
  107.3 4.7 %slice-start.4 = ((s8[8388608]{0:T(1024)(128)(4,1)}), s8[4194304]{0:T(1024)(128)(4,1)S(1)}, s32[]{:S(2)}) async-start(s8[8388608]{0:T(1024)(128)(4,1)} %bitcast.190), calls=%async_computation.6 | async-start | bytes 8388608
  107.3 3.2 %copy-start.7 = (bf16[1,1024,1024]{2,1,0:T(8,128)(2,1)S(1)}, bf16[1,1024,1024]{2,1,0:T(8,128)(2,1)}, u32[]{:S(2)}) copy-start(bf16[1,1024,1024]{2,1,0:T(8,128)(2,1)} %param.27) | copy-start | bytes 6291460
  107.3 3.2 %copy-start.9 = (bf16[256,1024]{1,0:T(8,128)(2,1)S(1)}, bf16[256,1024]{1,0:T(8,128)(2,1)}, u32[]{:S(2)}) copy-start(bf16[256,1024]{1,0:T(8,128)(2,1)} %reduce-scatter.2.cloned.1.call-done) | copy-start | bytes 1572868
  107.3 4.8 %slice-start.5 = ((s8[8388608]{0:T(1024)(128)(4,1)}), s8[4194304]{0:T(1024)(128)(4,1)S(1)}, s32[]{:S(2)}) async-start(s8[8388608]{0:T(1024)(128)(4,1)} %bitcast.190), calls=%async_computation.7 | async-start | bytes 8388608
  108.5 3.6 %slice-start.1 = ((f32[1,9216]{1,0:T(1,128)}), f32[1,4096]{1,0:T(1,128)S(1)}, s32[]{:S(2)}) async-start(f32[1,9216]{1,0:T(1,128)} %param.25), calls=%async_computation.3 | async-start | bytes 32768 | tf_op jit(solution)/shard_map/slice | solution.py:656
  111.2 3.9 %slice-start.2 = ((s8[8388608]{0:T(1024)(128)(4,1)}), s8[4194304]{0:T(1024)(128)(4,1)S(1)}, s32[]{:S(2)}) async-start(s8[8388608]{0:T(1024)(128)(4,1)} %bitcast.188), calls=%async_computation.4 | async-start | bytes 8388608
  111.7 3.4 %copy-start.4 = (f32[256,1024]{1,0:T(8,128)}, f32[256,1024]{1,0:T(8,128)S(1)}, u32[]{:S(2)}) copy-start(f32[256,1024]{1,0:T(8,128)S(1)} %get-tuple-element.44) | copy-start | bytes 3145732
  112.1 3.0 %slice-start.3 = ((s8[8388608]{0:T(1024)(128)(4,1)}), s8[4194304]{0:T(1024)(128)(4,1)S(1)}, s32[]{:S(2)}) async-start(s8[8388608]{0:T(1024)(128)(4,1)} %bitcast.188), calls=%async_computation.5 | async-start | bytes 8388608
  115.1 2.9 %copy-start.24 = (f32[256,4096]{1,0:T(8,128)}, f32[256,4096]{1,0:T(8,128)S(1)}, u32[]{:S(2)}) copy-start(f32[256,4096]{1,0:T(8,128)S(1)} %fusion.10) | copy-start | bytes 12582916
  118.0 1.0 copy-start.2
  220.9 14.8 %copy-start.3 = (f32[256,1024]{1,0:T(8,128)S(1)}, f32[256,1024]{1,0:T(8,128)}, u32[]{:S(2)}) copy-start(f32[256,1024]{1,0:T(8,128)} %copy-done.2) | copy-start | bytes 3145732
  220.9 14.8 %copy-start.5 = (f32[256,1024]{1,0:T(8,128)S(1)}, f32[256,1024]{1,0:T(8,128)}, u32[]{:S(2)}) copy-start(f32[256,1024]{1,0:T(8,128)} %copy-done.4) | copy-start | bytes 3145732
  235.7 2.8 copy-start.8
  239.8 5.1 %copy-start.17 = (bf16[256,1024]{0,1:T(8,128)(2,1)S(1)}, bf16[256,1024]{0,1:T(8,128)(2,1)}, u32[]{:S(2)}) copy-start(bf16[256,1024]{0,1:T(8,128)(2,1)} %copy-done.16) | copy-start | bytes 1572868
  241.7 3.5 %copy-start.1 = (f32[16,256,256]{1,2,0:T(8,128)S(1)}, f32[16,256,256]{1,2,0:T(8,128)}, u32[]{:S(2)}) copy-start(f32[16,256,256]{1,2,0:T(8,128)} %copy-done) | copy-start | bytes 12582916
  246.5 1.2 copy-start.15
  246.5 2.0 copy-start.13
  249.0 1.8 copy-start.11
Sparse Core Ops, SparseCore 0:
  41.7 52.3 reduce-scatter.1
